TPU v7x, 32 devices: a whole 2x2x4 slice. The times are simulated.
32 devices in a mesh: section: 4 (over y, core), tensor: 8 (over z, x).
Axes of the slice: x: 2, y: 2, z: 4, core: 2. Of those that a mesh axis runs over, the one named last changes fastest.
Arguments:
- saved_inputs: bfloat16 [4, 4, 256, 1024], P('section', None, 'tensor'), may hold values from -6 to 6
- slot_index: int32 [4, 3], P('section'), may hold values from 0 to 3
- example_lengths: int32 [4, 3, 2], P('section'), may hold values from 1 to 192, 256 in all within a row
- first_grads: bfloat16 [4, 256, 1024], P('section', 'tensor'), may hold values from -6 to 6
- loss_grads: bfloat16 [2, 256, 1024], P(None, 'tensor'), may hold values from -6 to 6
- w_in: bfloat16 [4, 1024, 32768], P('section', None, 'tensor'), may hold values from -0.1875 to 0.1875
- w_out: bfloat16 [4, 32768, 1024], P('section', 'tensor'), may hold values from -0.03125 to 0.03125
Outputs:
- grad_in: bfloat16 [4, 1024, 32768], P('section', None, 'tensor')
- grad_out: bfloat16 [4, 32768, 1024], P('section', 'tensor')
- input_grads: bfloat16 [4, 3, 256, 1024], P('section', None, 'tensor')
Inputs may be any that keep to these rules, and one draw needn't show every extreme that they name: `example_lengths`: the 2 lengths of one microbatch sum to 256.
All inputs are finite; a program needn't handle non-finite values.
Results may differ from a plain program's by a relative error of at most 0.0095.
Values may be sent and summed in bfloat16 or wider, within the bound.
A program may use at most 128 MiB of HBM per device.

v0:
```python
import jax
import jax.numpy as jnp
from jax import lax
from jax.sharding import PartitionSpec as P

D = 1024
FF = 32768


GAMMA = 0.01


def shifted(value, axis, steps):
    count = lax.axis_size(axis)
    first, last = (max(0, -steps), min(count, count - steps))
    return lax.ppermute(value, axis, [(source, source + steps) for source in range(first, last)])


def membership(lengths, tokens):
    ends = jnp.cumsum(lengths)
    position = jnp.arange(tokens, dtype=jnp.int32)
    example_id = jnp.sum((position[:, None] >= ends[None, :-1]).astype(jnp.int32), axis=1)
    labels = jnp.arange(lengths.shape[0], dtype=jnp.int32)
    return (example_id[:, None] == labels[None, :]).astype(jnp.float32)


def per_device(saved_inputs, slot_index, example_lengths, first_grads, loss_grads, w_in, w_out):
    section_count = lax.axis_size("section")
    is_last = lax.axis_index("section") == section_count - 1
    first = w_in[0]
    second = w_out[0]
    slot_count = loss_grads.shape[0] + 1
    rows = first_grads.shape[1]
    picked = [
        lax.dynamic_index_in_dim(saved_inputs[0], slot_index[0, slot], 0, keepdims=False)
        for slot in range(slot_count)
    ]
    every_input = lax.all_gather(jnp.stack(picked), "tensor", axis=1, tiled=True)
    acc_first = jnp.zeros(first.shape, jnp.float32)
    acc_second = jnp.zeros(second.shape, jnp.float32)
    incoming = first_grads[0]
    results = []
    for slot in range(slot_count):
        inputs = every_input[slot]
        grads = lax.all_gather(incoming, "tensor", axis=0, tiled=True)
        z = jnp.dot(inputs, first, preferred_element_type=jnp.float32)
        relu = jnp.maximum(z, 0.0)
        hidden = (relu * relu).astype(jnp.bfloat16)
        back = jnp.einsum("td,fd->tf", grads, second, preferred_element_type=jnp.float32)
        dz = (2.0 * relu * back).astype(jnp.bfloat16)
        own_terms = jnp.einsum("tf,df->td", dz, first, preferred_element_type=jnp.float32)
        summed = lax.psum(own_terms, "tensor")
        shares = lax.dynamic_slice_in_dim(summed, lax.axis_index("tensor") * rows, rows, 0)
        member = membership(example_lengths[0, slot], inputs.shape[0])
        pieces = []
        for example in range(member.shape[1]):
            keep = member[:, example][:, None].astype(jnp.bfloat16)
            per_first = jnp.einsum(
                "td,tf->df", inputs * keep, dz, preferred_element_type=jnp.float32
            )
            per_second = jnp.einsum(
                "tf,td->fd", hidden, grads * keep, preferred_element_type=jnp.float32
            )
            pieces.append(jnp.sum(per_first * per_first) + jnp.sum(per_second * per_second))
        local_squares = jnp.stack(pieces)
        squares = lax.psum(local_squares, "tensor")
        factor = 1.0 / (jnp.sqrt(squares / (D * FF)) + GAMMA)
        token_factor = jnp.sum(member * factor[None, :], axis=1)
        dzc = (dz.astype(jnp.float32) * token_factor[:, None]).astype(jnp.bfloat16)
        dyc = (grads.astype(jnp.float32) * token_factor[:, None]).astype(jnp.bfloat16)
        acc_first = acc_first + jnp.einsum(
            "td,tf->df", inputs, dzc, preferred_element_type=jnp.float32
        )
        acc_second = acc_second + jnp.einsum(
            "tf,td->fd", hidden, dyc, preferred_element_type=jnp.float32
        )
        passing = (incoming.astype(jnp.float32) + shares).astype(jnp.bfloat16)
        results.append(passing)
        if slot + 1 < slot_count:
            arrived = shifted(passing, "section", -1)
            incoming = jnp.where(is_last, loss_grads[slot], arrived)
    grad_in = acc_first.astype(jnp.bfloat16)[None]
    grad_out = acc_second.astype(jnp.bfloat16)[None]
    input_grads = jnp.stack(results)[None]
    return (grad_in, grad_out, input_grads)


def solution(mesh):
    return jax.shard_map(
        per_device,
        mesh=mesh,
        in_specs=(
            P("section", None, "tensor", None),
            P("section", None),
            P("section", None, None),
            P("section", "tensor", None),
            P(None, "tensor", None),
            P("section", None, "tensor"),
            P("section", "tensor", None),
        ),
        out_specs=(
            P("section", None, "tensor"),
            P("section", "tensor", None),
            P("section", None, "tensor", None),
        ),
        check_vma=False,
    )
```

profile of v0, /device:TPU:0, one launch (start us, length us, event | category | flops | bytes accessed | tf_op | source)
XLA Modules:
  0.0 492.7 jit_solution(11279649531270042013)
XLA Ops:
  17.9 34.1 %all-gather = bf16[1,256,1024]{2,1,0:T(8,128)(2,1)S(1)} all-gather(bf16[1,32,1024]{2,1,0:T(8,128)(2,1)} %param.10), channel_id=2, replica_groups=mesh['section'=4,'tensor'=8] {'tensor'}, dimensions={1}, use_global_device_ids=true | all-gather | bytes 589824 | tf_op jit(solution)/shard_map/all_gather | solution.py:45
  52.0 12.1 %all-gather.3.cloned.1.call-done = bf16[3,256,1024]{2,1,0:T(8,128)(2,1)} async-done(((bf16[3,32,1024]{2,1,0:T(8,128)(2,1)}), bf16[3,256,1024]{2,1,0:T(8,128)(2,1)}) %all-gather.3.cloned.1.call-update) | async-done | bytes 1572880 | tf_op jit(solution)/shard_map/all_gather | solution.py:38
  80.5 13.6 %fusion.44 = bf16[256,4096]{1,0:T(8,128)(2,1)S(1)} fusion(bf16[1,4096,1024]{2,1,0:T(8,128)(2,1)S(1)} %bitcast.137, f32[256,4096]{1,0:T(8,128)S(1)} %fusion.20, bf16[1,256,1024]{2,1,0:T(8,128)(2,1)S(1)} %all-gather), kind=kOutput, calls=%fused_computation.42 | convolution fusion | flops 2150629376 | bytes 15204352 | tf_op jit(solution)/shard_map/td,fd->tf/dot_general | solution.py:49
  94.1 7.5 %fusion.12 = f32[256,1024]{1,0:T(8,128)} fusion(bf16[256,4096]{1,0:T(8,128)(2,1)S(1)} %fusion.44, bf16[1,1024,4096]{2,1,0:T(8,128)(2,1)} %param.12), kind=kOutput, calls=%fused_computation.26 | convolution fusion | flops 2147483648 | bytes 11534336 | tf_op jit(solution)/shard_map/tf,df->td/dot_general | solution.py:51
  116.9 8.0 %fusion.26 = f32[256,4096]{1,0:T(8,128)} fusion(bf16[1,1024,4096]{2,1,0:T(8,128)(2,1)} %param.12, bf16[3,256,1024]{2,1,0:T(8,128)(2,1)} %all-gather.3.cloned.1.call-done), kind=kOutput, calls=%fused_computation.36 | convolution fusion | flops 2148532224 | bytes 13107200 | tf_op jit(solution)/shard_map/dot_general | solution.py:46
  124.9 8.5 %fusion.23 = f32[256,4096]{1,0:T(8,128)} fusion(bf16[1,1024,4096]{2,1,0:T(8,128)(2,1)} %param.12, bf16[3,256,1024]{2,1,0:T(8,128)(2,1)} %all-gather.3.cloned.1.call-done), kind=kOutput, calls=%fused_computation.35 | convolution fusion | flops 2148532224 | bytes 13107200 | tf_op jit(solution)/shard_map/dot_general | solution.py:46
  133.4 45.6 %all-reduce.5.cloned.1.call-done = f32[256,1024]{1,0:T(8,128)} async-done(((f32[256,1024]{1,0:T(8,128)}), f32[256,1024]{1,0:T(8,128)}) %all-reduce.5.cloned.1.call-update) | async-done | bytes 1048592 | tf_op jit(solution)/shard_map/psum | solution.py:52
  183.1 31.3 %all_gather.14 = bf16[256,1024]{1,0:T(8,128)(2,1)S(1)} all-gather(bf16[32,1024]{1,0:T(8,128)(2,1)S(1)} %bitcast_select_fusion.1), channel_id=1, replica_groups=mesh['section'=4,'tensor'=8] {'tensor'}, dimensions={0}, use_global_device_ids=true | all-gather | bytes 589824 | tf_op jit(solution)/shard_map/all_gather | solution.py:45
  214.4 7.2 %fusion.41 = bf16[256,4096]{1,0:T(8,128)(2,1)S(1)} fusion(bf16[256,1024]{1,0:T(8,128)(2,1)S(1)} %all_gather.14, bf16[1,4096,1024]{2,1,0:T(8,128)(2,1)} %param.13, f32[256,4096]{1,0:T(8,128)} %fusion.23), kind=kOutput, calls=%fused_computation.41 | convolution fusion | flops 2150629376 | bytes 15204352 | tf_op jit(solution)/shard_map/td,fd->tf/dot_general | solution.py:49
  226.8 6.8 %fusion.8 = f32[256,1024]{1,0:T(8,128)} fusion(bf16[256,4096]{1,0:T(8,128)(2,1)S(1)} %fusion.41, bf16[1,1024,4096]{2,1,0:T(8,128)(2,1)} %param.12), kind=kOutput, calls=%fused_computation.22 | convolution fusion | flops 2147483648 | bytes 11534336 | tf_op jit(solution)/shard_map/tf,df->td/dot_general | solution.py:51
  241.3 6.5 %multiply_reduce_fusion.7 = f32[]{:T(128)} fusion(bf16[256,4096]{1,0:T(8,128)(2,1)S(1)} %fusion.41, bf16[3,256,1024]{2,1,0:T(8,128)(2,1)} %all-gather.3.cloned.1.call-done, bf16[256]{0:T(256)(128)(2,1)S(1)} %get-tuple-element.8), kind=kOutput, calls=%fused_computation.9 | convolution fusion | flops 2156134400 | bytes 2621956 | tf_op jit(solution)/shard_map/td,tf->df/dot_general | solution.py:58
  254.7 57.6 %all-reduce.7.cloned.1.call-done = f32[256,1024]{1,0:T(8,128)} async-done(((f32[256,1024]{1,0:T(8,128)}), f32[256,1024]{1,0:T(8,128)}) %all-reduce.7.cloned.1.call-update) | async-done | bytes 1048592 | tf_op jit(solution)/shard_map/psum | solution.py:52
  316.4 31.3 %all_gather.15 = bf16[256,1024]{1,0:T(8,128)(2,1)S(1)} all-gather(bf16[32,1024]{1,0:T(8,128)(2,1)S(1)} %bitcast_select_fusion), channel_id=1, replica_groups=mesh['section'=4,'tensor'=8] {'tensor'}, dimensions={0}, use_global_device_ids=true | all-gather | bytes 589824 | tf_op jit(solution)/shard_map/all_gather | solution.py:45
  347.7 7.1 %fusion.38 = bf16[256,4096]{1,0:T(8,128)(2,1)S(1)} fusion(bf16[256,1024]{1,0:T(8,128)(2,1)S(1)} %all_gather.15, bf16[1,4096,1024]{2,1,0:T(8,128)(2,1)} %param.13, f32[256,4096]{1,0:T(8,128)} %fusion.26), kind=kOutput, calls=%fused_computation.40 | convolution fusion | flops 2150629376 | bytes 15204352 | tf_op jit(solution)/shard_map/td,fd->tf/dot_general | solution.py:49
  365.2 6.5 %multiply_reduce_fusion.1 = f32[]{:T(128)} fusion(bf16[256,4096]{1,0:T(8,128)(2,1)S(1)} %fusion.38, bf16[3,256,1024]{2,1,0:T(8,128)(2,1)} %all-gather.3.cloned.1.call-done, bf16[256]{0:T(256)(128)(2,1)S(1)} %get-tuple-element.4), kind=kOutput, calls=%fused_computation.3 | convolution fusion | flops 2156134400 | bytes 2621956 | tf_op jit(solution)/shard_map/td,tf->df/dot_general | solution.py:58
  373.0 6.3 %multiply_reduce_fusion.3 = f32[]{:T(128)} fusion(bf16[256,4096]{1,0:T(8,128)(2,1)S(1)} %fusion.38, bf16[3,256,1024]{2,1,0:T(8,128)(2,1)} %all-gather.3.cloned.1.call-done, bf16[256]{0:T(256)(128)(2,1)S(1)} %get-tuple-element.3), kind=kOutput, calls=%fused_computation.5 | convolution fusion | flops 2156134400 | bytes 2621956 | tf_op jit(solution)/shard_map/td,tf->df/dot_general | solution.py:58
  380.6 6.7 %fusion.6 = f32[256,1024]{1,0:T(8,128)} fusion(bf16[256,4096]{1,0:T(8,128)(2,1)S(1)} %fusion.38, bf16[1,1024,4096]{2,1,0:T(8,128)(2,1)} %param.12), kind=kOutput, calls=%fused_computation.20 | convolution fusion | flops 2147483648 | bytes 11534336 | tf_op jit(solution)/shard_map/tf,df->td/dot_general | solution.py:51
  387.3 20.4 %all-reduce = (f32[2]{0:T(128)S(1)}, f32[2]{0:T(128)S(1)}, f32[2]{0:T(128)S(1)}) all-reduce(f32[2]{0:T(128)S(1)} %pad_maximum_fusion.1, f32[2]{0:T(128)S(1)} %pad_maximum_fusion.2, f32[2]{0:T(128)S(1)} %pad_maximum_fusion.3), channel_id=1, replica_groups=mesh['section'=4,'tensor'=8] {'tensor'}, use_global_device_ids=true, to_apply=%region_5.6 | all-reduce | flops 6 | bytes 48 | tf_op jit(solution)/shard_map/psum | solution.py:66
  408.0 10.6 %fusion.53 = f32[4096,1024]{1,0:T(8,128)} fusion(bf16[256,1024]{1,0:T(8,128)(2,1)} %copy-done.5, f32[256]{0:T(256)S(1)} %select_reduce_fusion.1, f32[256,4096]{1,0:T(8,128)} %fusion.23), kind=kOutput, calls=%fused_computation.58 | convolution fusion | flops 2150367232 | bytes 21496832 | tf_op jit(solution)/shard_map/tf,td->fd/dot_general | solution.py:74
  418.7 8.2 %fusion.52 = f32[4096,1024]{1,0:T(8,128)} fusion(bf16[1,256,1024]{2,1,0:T(8,128)(2,1)S(1)} %all-gather, f32[256]{0:T(256)S(1)} %select_reduce_fusion.2, f32[256,4096]{1,0:T(8,128)S(1)} %copy-done.1), kind=kOutput, calls=%fused_computation.57 | convolution fusion | flops 2150367232 | bytes 21496832 | tf_op jit(solution)/shard_map/tf,td->fd/dot_general | solution.py:74
  426.9 16.7 %fusion.19 = bf16[1,4096,1024]{2,1,0:T(8,128)(2,1)} fusion(f32[4096,1024]{1,0:T(8,128)} %fusion.52, f32[4096,1024]{1,0:T(8,128)} %fusion.53, bf16[256,1024]{1,0:T(8,128)(2,1)S(1)} %all_gather.15, f32[256]{0:T(256)S(1)} %select_reduce_fusion, f32[256,4096]{1,0:T(8,128)} %fusion.26), kind=kOutput, calls=%fused_computation.33 | convolution fusion | flops 2162950144 | bytes 46662656 | tf_op jit(solution)/shard_map/tf,td->fd/dot_general | solution.py:74
  443.6 10.1 %fusion.47 = f32[1024,4096]{1,0:T(8,128)} fusion(bf16[256,4096]{1,0:T(8,128)(2,1)} %copy-done.6, f32[256]{0:T(256)S(1)} %select_reduce_fusion.2, bf16[3,256,1024]{2,1,0:T(8,128)(2,1)} %all-gather.3.cloned.1.call-done), kind=kOutput, calls=%fused_computation.49 | convolution fusion | flops 2150629376 | bytes 19399680 | tf_op jit(solution)/shard_map/td,tf->df/dot_general | solution.py:71
  453.7 9.3 %fusion.48 = f32[1024,4096]{1,0:T(8,128)} fusion(bf16[256,4096]{1,0:T(8,128)(2,1)S(1)} %copy-done.8, f32[256]{0:T(256)S(1)} %select_reduce_fusion.1, bf16[3,256,1024]{2,1,0:T(8,128)(2,1)} %all-gather.3.cloned.1.call-done), kind=kOutput, calls=%fused_computation.50 | convolution fusion | flops 2150629376 | bytes 19399680 | tf_op jit(solution)/shard_map/td,tf->df/dot_general | solution.py:71
  463.0 16.0 %fusion.18 = bf16[1,1024,4096]{2,1,0:T(8,128)(2,1)} fusion(f32[1024,4096]{1,0:T(8,128)} %fusion.47, f32[1024,4096]{1,0:T(8,128)} %fusion.48, bf16[256,4096]{1,0:T(8,128)(2,1)S(1)} %fusion.38, f32[256]{0:T(256)S(1)} %select_reduce_fusion, bf16[3,256,1024]{2,1,0:T(8,128)(2,1)} %all-gather.3.cloned.1.call-done), kind=kOutput, calls=%fused_computation.32 | convolution fusion | flops 2163212288 | bytes 44565504 | tf_op jit(solution)/shard_map/td,tf->df/dot_general | solution.py:71
  (80 shorter events, 76.9 us)
Async XLA Ops:
  7.2 56.9 %all-gather.3.cloned.1.call-start = ((), (), s32[]{:S(2)}) async-start(), calls=%async_computation | async-start | bytes 1769472 | tf_op jit(solution)/shard_map/all_gather | solution.py:38
  16.1 162.9 %all-reduce.5.cloned.1.call-start = ((), (), s32[]{:S(2)}) async-start(), calls=%async_computation.1 | async-start | bytes 2097152 | tf_op jit(solution)/shard_map/psum | solution.py:52
  70.0 10.4 %copy-start = (f32[256,4096]{1,0:T(8,128)}, f32[256,4096]{1,0:T(8,128)S(1)}, u32[]{:S(2)}) copy-start(f32[256,4096]{1,0:T(8,128)S(1)} %fusion.20) | copy-start | bytes 12582916
  70.1 10.4 %slice-start = ((s8[8388608]{0:T(1024)(128)(4,1)}), s8[4194304]{0:T(1024)(128)(4,1)S(1)}, s32[]{:S(2)}) async-start(s8[8388608]{0:T(1024)(128)(4,1)} %bitcast.136), calls=%async_computation.4 | async-start | bytes 8388608
  75.3 5.2 %slice-start.1 = ((s8[8388608]{0:T(1024)(128)(4,1)}), s8[4194304]{0:T(1024)(128)(4,1)S(1)}, s32[]{:S(2)}) async-start(s8[8388608]{0:T(1024)(128)(4,1)} %bitcast.136), calls=%async_computation.5 | async-start | bytes 8388608
  94.1 15.2 %copy-start.6 = (bf16[256,4096]{1,0:T(8,128)(2,1)}, bf16[256,4096]{1,0:T(8,128)(2,1)S(1)}, u32[]{:S(2)}) copy-start(bf16[256,4096]{1,0:T(8,128)(2,1)S(1)} %fusion.44) | copy-start | bytes 6291460
  101.6 210.7 %all-reduce.7.cloned.1.call-start = ((), (), s32[]{:S(2)}) async-start(), calls=%async_computation.2 | async-start | bytes 2097152 | tf_op jit(solution)/shard_map/psum | solution.py:52
  124.9 54.1 %copy-start.9 = (bf16[1,32,1024]{2,1,0:T(8,128)(2,1)S(1)}, bf16[1,32,1024]{2,1,0:T(8,128)(2,1)}, u32[]{:S(2)}) copy-start(bf16[1,32,1024]{2,1,0:T(8,128)(2,1)} %param.10) | copy-start | bytes 196612
  124.9 58.2 %copy-start.10 = (bf16[2,32,1024]{2,1,0:T(8,128)(2,1)S(1)}, bf16[2,32,1024]{2,1,0:T(8,128)(2,1)}, u32[]{:S(2)}) copy-start(bf16[2,32,1024]{2,1,0:T(8,128)(2,1)} %param.11) | copy-start | bytes 393220
  179.9 3.1 collective-permute-start
  214.4 33.5 %copy-start.5 = (bf16[256,1024]{1,0:T(8,128)(2,1)}, bf16[256,1024]{1,0:T(8,128)(2,1)S(1)}, u32[]{:S(2)}) copy-start(bf16[256,1024]{1,0:T(8,128)(2,1)S(1)} %all_gather.14) | copy-start | bytes 1572868
  214.4 7.2 %copy-start.2 = (f32[256,4096]{1,0:T(8,128)S(1)}, f32[256,4096]{1,0:T(8,128)}, u32[]{:S(2)}) copy-start(f32[256,4096]{1,0:T(8,128)} %fusion.23) | copy-start | bytes 12582916
  221.6 19.7 %copy-start.7 = (bf16[256,4096]{1,0:T(8,128)(2,1)}, bf16[256,4096]{1,0:T(8,128)(2,1)S(1)}, u32[]{:S(2)}) copy-start(bf16[256,4096]{1,0:T(8,128)(2,1)S(1)} %fusion.41) | copy-start | bytes 6291460
  233.6 250.6 %all-reduce.9.cloned.1.call-start = ((), (), s32[]{:S(2)}) async-start(), calls=%async_computation.3 | async-start | bytes 2097152 | tf_op jit(solution)/shard_map/psum | solution.py:52
  241.3 6.5 %copy-start.3 = (f32[256,4096]{1,0:T(8,128)S(1)}, f32[256,4096]{1,0:T(8,128)}, u32[]{:S(2)}) copy-start(f32[256,4096]{1,0:T(8,128)} %fusion.23) | copy-start | bytes 12582916
  313.2 3.1 collective-permute-start.1
  347.7 7.1 %copy-start.4 = (f32[256,4096]{1,0:T(8,128)S(1)}, f32[256,4096]{1,0:T(8,128)}, u32[]{:S(2)}) copy-start(f32[256,4096]{1,0:T(8,128)} %fusion.26) | copy-start | bytes 12582916
  408.0 10.6 %copy-start.1 = (f32[256,4096]{1,0:T(8,128)S(1)}, f32[256,4096]{1,0:T(8,128)}, u32[]{:S(2)}) copy-start(f32[256,4096]{1,0:T(8,128)} %copy-done) | copy-start | bytes 12582916
  443.6 10.1 %copy-start.8 = (bf16[256,4096]{1,0:T(8,128)(2,1)S(1)}, bf16[256,4096]{1,0:T(8,128)(2,1)}, u32[]{:S(2)}) copy-start(bf16[256,4096]{1,0:T(8,128)(2,1)} %copy-done.7) | copy-start | bytes 6291460
Sparse Core Ops, SparseCore 0:
  16.2 47.8 all-gather.2
  101.7 77.2 all-reduce.4
  233.7 78.5 all-reduce.6
  408.1 75.9 all-reduce.8
where the time goes:
time: 497 us; the launch traced here: 493 us
  matrix products  212 us (43%)
  waiting for transfers between devices  124 us (25%)
  blocking collectives  117 us (24%)
  between operations  27.8 us (6%)
  other arithmetic  5.36 us (1%)
    psum x3, waiting for transfers between devices, per_device(): summed = lax.psum(own_terms, 'tensor')  108 us
    all_gather x3, blocking collectives, per_device(): grads = lax.all_gather(incoming, 'tensor', axis=0, tiled=True)  96.7 us
    dot_general x6, matrix products, per_device(): jnp.einsum('td,tf->df', inputs * keep, dz, preferred_element_type=jnp.flo...  38.2 us
    dot_general x3, matrix products, per_device(): jnp.einsum('tf,td->fd', hidden, dyc, preferred_element_type=jnp.float32)  35.6 us
    dot_general x3, matrix products, per_device(): jnp.einsum('td,tf->df', inputs, dzc, preferred_element_type=jnp.float32)  35.4 us
    dot_general x6, matrix products, per_device(): jnp.einsum('tf,td->fd', hidden, grads * keep, preferred_element_type=jnp....  31.6 us
    dot_general x3, matrix products, per_device(): jnp.einsum('td,fd->tf', grads, second, preferred_element_type=jnp.float32)  27.9 us
    dot_general x3, matrix products, per_device(): z = jnp.dot(inputs, first, preferred_element_type=jnp.float32)  22.4 us
  transfers between devices with their start and end apart: 6, of which 6 were waited for; matrix products, arithmetic and copies ran while one was open for 24% of the time, Pallas kernels for 0%

commit v1 on v0

v1 whole, which is shorter than its diff:
```python
import jax
import jax.numpy as jnp
from jax import lax
from jax.sharding import PartitionSpec as P

GAMMA = 0.01
F32 = jnp.float32
BF16 = jnp.bfloat16


def shifted(value, axis, steps):
    count = lax.axis_size(axis)
    first, last = (max(0, -steps), min(count, count - steps))
    return lax.ppermute(value, axis, [(source, source + steps) for source in range(first, last)])


def membership(lengths, tokens):
    ends = jnp.cumsum(lengths)
    position = jnp.arange(tokens, dtype=jnp.int32)
    example_id = jnp.sum((position[:, None] >= ends[None, :-1]).astype(jnp.int32), axis=1)
    labels = jnp.arange(lengths.shape[0], dtype=jnp.int32)
    return (example_id[:, None] == labels[None, :]).astype(F32)


def spread(value, axis):
    copies = jnp.broadcast_to(value[None], (lax.axis_size(axis),) + value.shape)
    return lax.all_to_all(copies, axis, 0, 0)


def gram(value):
    return lax.dot_general(value, value, (((1,), (1,)), ((), ())), preferred_element_type=F32)


def per_device(saved_inputs, slot_index, example_lengths, first_grads, loss_grads, w_in, w_out):
    section_count = lax.axis_size("section")
    parts = lax.axis_size("tensor")
    is_last = lax.axis_index("section") == section_count - 1
    first = w_in[0]
    second = w_out[0]
    slot_count = loss_grads.shape[0] + 1
    rows, width = first_grads.shape[1:]
    hidden_all = first.shape[1] * parts
    picked = [
        lax.dynamic_index_in_dim(saved_inputs[0], slot_index[0, slot], 0, keepdims=False)
        for slot in range(slot_count)
    ]
    tokens = parts * rows
    opening = spread(jnp.concatenate([picked[0], first_grads[0]]), "tensor")
    later = spread(jnp.concatenate(picked[1:]), "tensor")
    every_input = [opening[:, :rows].reshape(tokens, width)]
    for slot in range(slot_count - 1):
        every_input.append(later[:, slot * rows : (slot + 1) * rows].reshape(tokens, width))
    incoming = first_grads[0]
    results, dzs, hiddens, grad_list, members, squares = [], [], [], [], [], []
    for slot in range(slot_count):
        inputs = every_input[slot]
        if slot == 0:
            grads = opening[:, rows:].reshape(tokens, width)
        else:
            grads = spread(incoming, "tensor").reshape(tokens, width)
        z = jnp.dot(inputs, first, preferred_element_type=F32)
        relu = jnp.maximum(z, 0.0)
        hidden = (relu * relu).astype(BF16)
        back = jnp.einsum("td,fd->tf", grads, second, preferred_element_type=F32)
        dz = (2.0 * relu * back).astype(BF16)
        own_terms = jnp.einsum("tf,df->td", dz, first, preferred_element_type=F32).astype(BF16)
        pieces = lax.all_to_all(own_terms.reshape(parts, rows, width), "tensor", 0, 0)
        shares = jnp.sum(pieces.astype(F32), axis=0)
        passing = (incoming.astype(F32) + shares).astype(BF16)
        results.append(passing)
        if slot + 1 < slot_count:
            arrived = shifted(passing, "section", -1)
            incoming = jnp.where(is_last, loss_grads[slot], arrived)
        member = membership(example_lengths[0, slot], inputs.shape[0])
        paired = gram(inputs) * gram(dz) + gram(hidden) * gram(grads)
        per_row = jnp.stack([jnp.sum(paired * member[:, e][None, :], axis=1) for e in range(member.shape[1])], axis=1)
        squares.append(jnp.sum(member * per_row, axis=0))
        dzs.append(dz)
        hiddens.append(hidden)
        grad_list.append(grads)
        members.append(member)
    local = jnp.stack(squares)
    total = jnp.sum(spread(local, "tensor"), axis=0)
    factor = 1.0 / (jnp.sqrt(total / (width * hidden_all)) + GAMMA)
    token_factor = jnp.concatenate([jnp.sum(m * factor[i][None, :], axis=1) for i, m in enumerate(members)])[:, None]
    xc = (jnp.concatenate(every_input).astype(F32) * token_factor).astype(BF16)
    dyc = (jnp.concatenate(grad_list).astype(F32) * token_factor).astype(BF16)
    grad_in = jnp.einsum("td,tf->df", xc, jnp.concatenate(dzs), preferred_element_type=F32).astype(BF16)[None]
    grad_out = jnp.einsum("tf,td->fd", jnp.concatenate(hiddens), dyc, preferred_element_type=F32).astype(BF16)[None]
    input_grads = jnp.stack(results)[None]
    return (grad_in, grad_out, input_grads)


def solution(mesh):
    return jax.shard_map(
        per_device,
        mesh=mesh,
        in_specs=(
            P("section", None, "tensor", None),
            P("section", None),
            P("section", None, None),
            P("section", "tensor", None),
            P(None, "tensor", None),
            P("section", None, "tensor"),
            P("section", "tensor", None),
        ),
        out_specs=(
            P("section", None, "tensor"),
            P("section", "tensor", None),
            P("section", None, "tensor", None),
        ),
        check_vma=False,
    )
```

time: 497 us -> 229 us (0.46)
  blocking collectives: 117 us -> 0 us
  matrix products: 212 us -> 95.6 us
  waiting for transfers between devices: 124 us -> 58.6 us
  starting transfers between devices: 2.93 us -> 41 us
  between operations: 27.8 us -> 7.11 us
  local copies, waits for them, and re-layouts: 3.42 us -> 15.4 us
    dot_general x27 -> x23, matrix products: 212 us -> 95.6 us  [the longest x3 24.7 us: per_device(): z = jnp.dot(inputs, first, preferred_element_type=F32)]
    psum x3 -> x0, waiting for transfers between devices: 108 us -> none  [per_device(): summed = lax.psum(own_terms, 'tensor')]
    all_gather x3 -> x0, blocking collectives: 96.7 us -> none  [per_device(): grads = lax.all_gather(incoming, 'tensor', axis=0, tiled=True)]
    all_to_all x0 -> x8, waiting for transfers between devices: none -> 57.5 us  [the longest x5 44.8 us: spread(): return lax.all_to_all(copies, axis, 0, 0)]
    all_to_all x0 -> x8, starting transfers between devices: none -> 38.4 us  [the longest x5 23.7 us: spread(): return lax.all_to_all(copies, axis, 0, 0)]
    psum x1 -> x0, blocking collectives: 20.4 us -> none  [per_device(): squares = lax.psum(local_squares, 'tensor')]
    all_gather x1 -> x0, waiting for transfers between devices: 12.1 us -> none  [per_device(): lax.all_gather(jnp.stack(picked), 'tensor', axis=1, tiled=True)]
  transfers between devices with their start and end apart: 6 -> 10, of which waited for: 6 -> 7; matrix products, arithmetic and copies ran while one was open for 24% -> 35% of each run, Pallas kernels for 0% -> 0%
where the time goes in v1:
time: 229 us; the launch traced here: 228 us
  matrix products  95.6 us (42%)
  waiting for transfers between devices  58.6 us (26%)
  starting transfers between devices  41 us (18%)
  local copies, waits for them, and re-layouts  15.4 us (7%)
  other arithmetic  10.1 us (4%)
  between operations  7.11 us (3%)
    all_to_all x5, waiting for transfers between devices, spread(): return lax.all_to_all(copies, axis, 0, 0)  44.8 us
    dot_general x3, matrix products, per_device(): z = jnp.dot(inputs, first, preferred_element_type=F32)  24.7 us
    all_to_all x5, starting transfers between devices, spread(): return lax.all_to_all(copies, axis, 0, 0)  23.7 us
    dot_general x3, matrix products, per_device(): back = jnp.einsum('td,fd->tf', grads, second, preferred_element_type=F32)  18.7 us
    dot_general x3, matrix products, per_device(): jnp.einsum('tf,df->td', dz, first, preferred_element_type=F32).astype(BF16)  17.7 us
    all_to_all x3, starting transfers between devices, per_device(): lax.all_to_all(own_terms.reshape(parts, rows, width), 'tensor', 0, 0)  14.7 us
    dot_general x12, matrix products, gram(): lax.dot_general(value, value, (((1,), (1,)), ((), ())), preferred_element...  13.9 us
    all_to_all x3, waiting for transfers between devices, per_device(): lax.all_to_all(own_terms.reshape(parts, rows, width), 'tensor', 0, 0)  12.7 us
  transfers between devices with their start and end apart: 10, of which 7 were waited for; matrix products, arithmetic and copies ran while one was open for 35% of the time, Pallas kernels for 0%

profile of v1, /device:TPU:0, one launch (start us, length us, event | category | flops | bytes accessed | tf_op | source)
XLA Modules:
  0.0 227.8 jit_solution(14259533319539249769)
XLA Ops:
  10.7 7.3 %all-to-all-start = ((bf16[8,64,1024]{2,1,0:T(8,128)(2,1)}), bf16[8,64,1024]{2,1,0:T(8,128)(2,1)S(1)}, u32[]{:S(2)}, u32[]{:S(2)}) async-start(bf16[8,64,1024]{2,1,0:T(8,128)(2,1)} %broadcast_in_dim.16), calls=%async_computation | async-start | bytes 2097152 | tf_op jit(solution)/shard_map/all_to_all | solution.py:27
  20.6 23.1 %all-to-all-done = bf16[8,64,1024]{2,1,0:T(8,128)(2,1)S(1)} async-done(((bf16[8,64,1024]{2,1,0:T(8,128)(2,1)}), bf16[8,64,1024]{2,1,0:T(8,128)(2,1)S(1)}, u32[]{:S(2)}, u32[]{:S(2)}) %all-to-all-start) | async-done | bytes 1048608 | tf_op jit(solution)/shard_map/all_to_all | solution.py:27
  44.9 4.2 %all-to-all-start.1 = ((bf16[8,64,1024]{2,1,0:T(8,128)(2,1)}), bf16[8,64,1024]{2,1,0:T(8,128)(2,1)}, u32[]{:S(2)}, u32[]{:S(2)}) async-start(bf16[8,64,1024]{2,1,0:T(8,128)(2,1)} %broadcast_in_dim.17), calls=%async_computation.1 | async-start | bytes 2097152 | tf_op jit(solution)/shard_map/all_to_all | solution.py:27
  49.3 8.9 %multiply_convert_fusion.2 = (bf16[256,4096]{1,0:T(8,128)(2,1)}, f32[256,4096]{1,0:T(8,128)}) fusion(bf16[256,1024]{1,0:T(8,128)(2,1)S(1)} %bitcast.150, bf16[1,1024,4096]{2,1,0:T(8,128)(2,1)} %param.12), kind=kOutput, calls=%fused_computation.41 | convolution fusion | flops 2150629376 | bytes 15204352 | tf_op jit(solution)/shard_map/dot_general | solution.py:61
  58.3 4.8 %fusion.52 = bf16[256,4096]{1,0:T(8,128)(2,1)S(1)} fusion(bf16[256,1024]{1,0:T(8,128)(2,1)S(1)} %bitcast.153, bf16[1,4096,1024]{2,1,0:T(8,128)(2,1)S(1)} %bitcast.186, f32[256,4096]{1,0:T(8,128)} %get-tuple-element.36), kind=kOutput, calls=%fused_computation.38 | convolution fusion | flops 2150629376 | bytes 15204352 | tf_op jit(solution)/shard_map/td,fd->tf/dot_general | solution.py:64
  66.2 8.5 %all-to-all-done.1 = bf16[8,64,1024]{2,1,0:T(8,128)(2,1)} async-done(((bf16[8,64,1024]{2,1,0:T(8,128)(2,1)}), bf16[8,64,1024]{2,1,0:T(8,128)(2,1)}, u32[]{:S(2)}, u32[]{:S(2)}) %all-to-all-start.1) | async-done | bytes 1048608 | tf_op jit(solution)/shard_map/all_to_all | solution.py:27
  74.8 4.1 %all-to-all-start.2 = ((bf16[8,32,1024]{2,1,0:T(8,128)(2,1)}), bf16[8,32,1024]{2,1,0:T(8,128)(2,1)}, u32[]{:S(2)}, u32[]{:S(2)}) async-start(bf16[8,32,1024]{2,1,0:T(8,128)(2,1)} %bitcast.164), calls=%async_computation.2 | async-start | bytes 1048576 | tf_op jit(solution)/shard_map/all_to_all | solution.py:67
  85.8 7.2 %all-to-all-done.2 = bf16[8,32,1024]{2,1,0:T(8,128)(2,1)} async-done(((bf16[8,32,1024]{2,1,0:T(8,128)(2,1)}), bf16[8,32,1024]{2,1,0:T(8,128)(2,1)}, u32[]{:S(2)}, u32[]{:S(2)}) %all-to-all-start.2) | async-done | bytes 524320 | tf_op jit(solution)/shard_map/all_to_all | solution.py:67
  100.5 3.7 %all-to-all-start.3 = ((bf16[8,32,1024]{2,1,0:T(8,128)(2,1)}), bf16[8,32,1024]{2,1,0:T(8,128)(2,1)S(1)}, u32[]{:S(2)}, u32[]{:S(2)}) async-start(bf16[8,32,1024]{2,1,0:T(8,128)(2,1)} %broadcast_in_dim.18), calls=%async_computation.3 | async-start | bytes 1048576 | tf_op jit(solution)/shard_map/all_to_all | solution.py:27
  104.2 8.0 %multiply_convert_fusion.1 = (bf16[256,4096]{1,0:T(8,128)(2,1)S(1)}, f32[256,4096]{1,0:T(8,128)}) fusion(bf16[256,1024]{1,0:T(8,128)(2,1)} %bitcast.159, bf16[1,1024,4096]{2,1,0:T(8,128)(2,1)} %param.12), kind=kOutput, calls=%fused_computation.40 | convolution fusion | flops 2150629376 | bytes 15204352 | tf_op jit(solution)/shard_map/dot_general | solution.py:61
  115.0 4.1 %all-to-all-done.3 = bf16[8,32,1024]{2,1,0:T(8,128)(2,1)S(1)} async-done(((bf16[8,32,1024]{2,1,0:T(8,128)(2,1)}), bf16[8,32,1024]{2,1,0:T(8,128)(2,1)S(1)}, u32[]{:S(2)}, u32[]{:S(2)}) %all-to-all-start.3) | async-done | bytes 524320 | tf_op jit(solution)/shard_map/all_to_all | solution.py:27
  119.0 6.9 %fusion.49 = bf16[256,4096]{1,0:T(8,128)(2,1)S(1)} fusion(bf16[256,1024]{1,0:T(8,128)(2,1)S(1)} %bitcast.144, bf16[1,4096,1024]{2,1,0:T(8,128)(2,1)} %param.13, f32[256,4096]{1,0:T(8,128)} %get-tuple-element.34), kind=kOutput, calls=%fused_computation.37 | convolution fusion | flops 2150629376 | bytes 15204352 | tf_op jit(solution)/shard_map/td,fd->tf/dot_general | solution.py:64
  126.0 7.3 %fusion.70 = bf16[256,1024]{1,0:T(8,128)(2,1)} fusion(bf16[256,4096]{1,0:T(8,128)(2,1)S(1)} %fusion.49, bf16[1,1024,4096]{2,1,0:T(8,128)(2,1)} %param.12), kind=kOutput, calls=%fused_computation.57 | convolution fusion | flops 2147745792 | bytes 11010048 | tf_op jit(solution)/shard_map/tf,df->td/dot_general | solution.py:66
  133.3 4.6 %all-to-all-start.4 = ((bf16[8,32,1024]{2,1,0:T(8,128)(2,1)}), bf16[8,32,1024]{2,1,0:T(8,128)(2,1)}, u32[]{:S(2)}, u32[]{:S(2)}) async-start(bf16[8,32,1024]{2,1,0:T(8,128)(2,1)} %bitcast.165), calls=%async_computation.4 | async-start | bytes 1048576 | tf_op jit(solution)/shard_map/all_to_all | solution.py:67
  137.9 7.8 %multiply_convert_fusion = (bf16[256,4096]{1,0:T(8,128)(2,1)S(1)}, f32[256,4096]{1,0:T(8,128)}) fusion(bf16[256,1024]{1,0:T(8,128)(2,1)S(1)} %bitcast.156, bf16[1,1024,4096]{2,1,0:T(8,128)(2,1)} %param.12), kind=kOutput, calls=%fused_computation.39 | convolution fusion | flops 2150629376 | bytes 15204352 | tf_op jit(solution)/shard_map/dot_general | solution.py:61
  147.8 5.5 %all-to-all-done.4 = bf16[8,32,1024]{2,1,0:T(8,128)(2,1)} async-done(((bf16[8,32,1024]{2,1,0:T(8,128)(2,1)}), bf16[8,32,1024]{2,1,0:T(8,128)(2,1)}, u32[]{:S(2)}, u32[]{:S(2)}) %all-to-all-start.4) | async-done | bytes 524320 | tf_op jit(solution)/shard_map/all_to_all | solution.py:67
  158.5 3.7 %all-to-all-start.5 = ((bf16[8,32,1024]{2,1,0:T(8,128)(2,1)}), bf16[8,32,1024]{2,1,0:T(8,128)(2,1)S(1)}, u32[]{:S(2)}, u32[]{:S(2)}) async-start(bf16[8,32,1024]{2,1,0:T(8,128)(2,1)} %broadcast_in_dim.19), calls=%async_computation.5 | async-start | bytes 1048576 | tf_op jit(solution)/shard_map/all_to_all | solution.py:27
  167.6 9.1 %all-to-all-done.5 = bf16[8,32,1024]{2,1,0:T(8,128)(2,1)S(1)} async-done(((bf16[8,32,1024]{2,1,0:T(8,128)(2,1)}), bf16[8,32,1024]{2,1,0:T(8,128)(2,1)S(1)}, u32[]{:S(2)}, u32[]{:S(2)}) %all-to-all-start.5) | async-done | bytes 524320 | tf_op jit(solution)/shard_map/all_to_all | solution.py:27
  176.8 6.9 %fusion.46 = bf16[256,4096]{1,0:T(8,128)(2,1)S(1)} fusion(bf16[256,1024]{1,0:T(8,128)(2,1)S(1)} %bitcast.147, bf16[1,4096,1024]{2,1,0:T(8,128)(2,1)} %param.13, f32[256,4096]{1,0:T(8,128)} %get-tuple-element.32), kind=kOutput, calls=%fused_computation.36 | convolution fusion | flops 2150629376 | bytes 15204352 | tf_op jit(solution)/shard_map/td,fd->tf/dot_general | solution.py:64
  186.7 4.8 %all-to-all-start.6 = ((f32[8,3,2]{1,2,0:T(2,128)}), f32[8,3,2]{1,2,0:T(2,128)S(1)}, u32[]{:S(2)}, u32[]{:S(2)}) async-start(f32[8,3,2]{1,2,0:T(2,128)} %broadcast_in_dim.20), calls=%async_computation.6 | async-start | bytes 16384 | tf_op jit(solution)/shard_map/all_to_all | solution.py:27
  191.5 7.2 %fusion.73 = bf16[256,1024]{1,0:T(8,128)(2,1)} fusion(bf16[256,4096]{1,0:T(8,128)(2,1)} %copy-done.4, bf16[1,1024,4096]{2,1,0:T(8,128)(2,1)} %param.12), kind=kOutput, calls=%fused_computation.58 | convolution fusion | flops 2147745792 | bytes 11010048 | tf_op jit(solution)/shard_map/tf,df->td/dot_general | solution.py:66
  198.7 6.0 %all-to-all-start.7 = ((bf16[8,32,1024]{2,1,0:T(8,128)(2,1)}), bf16[8,32,1024]{2,1,0:T(8,128)(2,1)}, u32[]{:S(2)}, u32[]{:S(2)}) async-start(bf16[8,32,1024]{2,1,0:T(8,128)(2,1)} %bitcast.163), calls=%async_computation.7 | async-start | bytes 1048576 | tf_op jit(solution)/shard_map/all_to_all | solution.py:67
  205.2 11.3 %convert_bitcast_fusion = bf16[1,4096,1024]{2,1,0:T(8,128)(2,1)} fusion(bf16[256,4096]{1,0:T(8,128)(2,1)} %copy-done.3, bf16[256,4096]{1,0:T(8,128)(2,1)} %copy-done, bf16[256,4096]{1,0:T(8,128)(2,1)} %get-tuple-element.35, bf16[256,1024]{1,0:T(8,128)(2,1)S(1)} %bitcast.149, bf16[256,1024]{1,0:T(8,128)(2,1)S(1)} %bitcast.146, ...), kind=kOutput, calls=%fused_computation.18 | convolution fusion | flops 6471811072 | bytes 16256000 | tf_op jit(solution)/shard_map/tf,td->fd/dot_general | solution.py:89
  216.5 9.4 %convert_bitcast_fusion.1 = bf16[1,1024,4096]{2,1,0:T(8,128)(2,1)} fusion(bf16[256,4096]{1,0:T(8,128)(2,1)S(1)} %copy-done.5, bf16[256,4096]{1,0:T(8,128)(2,1)S(1)} %copy-done.2, bf16[256,4096]{1,0:T(8,128)(2,1)S(1)} %fusion.52, bf16[256,1024]{1,0:T(8,128)(2,1)S(1)} %bitcast.158, bf16[256,1024]{1,0:T(8,128)(2,1)S(1)} %bitcast.161, ...), kind=kOutput, calls=%fused_computation.19 | convolution fusion | flops 6471811072 | bytes 16256000 | tf_op jit(solution)/shard_map/td,tf->df/dot_general | solution.py:88
  (134 shorter events, 46.2 us)
Async XLA Ops:
  0.6 17.4 %copy-start.23 = (s32[1,3,2]{1,2,0:T(2,128)S(1)}, s32[1,3,2]{1,2,0:T(2,128)}, u32[]{:S(2)}) copy-start(s32[1,3,2]{1,2,0:T(2,128)} %param.9) | copy-start | bytes 76
  10.7 33.1 %all-to-all-start = ((bf16[8,64,1024]{2,1,0:T(8,128)(2,1)}), bf16[8,64,1024]{2,1,0:T(8,128)(2,1)S(1)}, u32[]{:S(2)}, u32[]{:S(2)}) async-start(bf16[8,64,1024]{2,1,0:T(8,128)(2,1)} %broadcast_in_dim.16), calls=%async_computation | async-start | bytes 2097152 | tf_op jit(solution)/shard_map/all_to_all | solution.py:27
  44.9 29.8 %all-to-all-start.1 = ((bf16[8,64,1024]{2,1,0:T(8,128)(2,1)}), bf16[8,64,1024]{2,1,0:T(8,128)(2,1)}, u32[]{:S(2)}, u32[]{:S(2)}) async-start(bf16[8,64,1024]{2,1,0:T(8,128)(2,1)} %broadcast_in_dim.17), calls=%async_computation.1 | async-start | bytes 2097152 | tf_op jit(solution)/shard_map/all_to_all | solution.py:27
  49.3 32.6 %copy-start.8 = (bf16[8,32,1024]{2,1,0:T(8,128)(2,1)}, bf16[8,32,1024]{2,1,0:T(8,128)(2,1)S(1)}, u32[]{:S(2)}) copy-start(bf16[8,32,1024]{2,1,0:T(8,128)(2,1)S(1)} %get-tuple-element.18) | copy-start | bytes 1572868
  49.3 47.0 %copy-start.6 = (bf16[8,32,1024]{2,1,0:T(8,128)(2,1)}, bf16[8,32,1024]{2,1,0:T(8,128)(2,1)S(1)}, u32[]{:S(2)}) copy-start(bf16[8,32,1024]{2,1,0:T(8,128)(2,1)S(1)} %get-tuple-element.17) | copy-start | bytes 1572868
  49.3 13.8 %slice-start.2 = ((s8[8388608]{0:T(1024)(128)(4,1)}), s8[4194304]{0:T(1024)(128)(4,1)S(1)}, s32[]{:S(2)}) async-start(s8[8388608]{0:T(1024)(128)(4,1)} %bitcast.187), calls=%async_computation.10 | async-start | bytes 8388608
  74.8 18.3 %all-to-all-start.2 = ((bf16[8,32,1024]{2,1,0:T(8,128)(2,1)}), bf16[8,32,1024]{2,1,0:T(8,128)(2,1)}, u32[]{:S(2)}, u32[]{:S(2)}) async-start(bf16[8,32,1024]{2,1,0:T(8,128)(2,1)} %bitcast.164), calls=%async_computation.2 | async-start | bytes 1048576 | tf_op jit(solution)/shard_map/all_to_all | solution.py:67
  85.1 52.8 %copy-start.9 = (bf16[8,32,1024]{2,1,0:T(8,128)(2,1)}, bf16[8,32,1024]{2,1,0:T(8,128)(2,1)S(1)}, u32[]{:S(2)}) copy-start(bf16[8,32,1024]{2,1,0:T(8,128)(2,1)S(1)} %get-tuple-element.15) | copy-start | bytes 1572868
  95.0 3.2 %collective-permute-start = (bf16[32,1024]{1,0:T(8,128)(2,1)S(1)}, bf16[32,1024]{1,0:T(8,128)(2,1)S(1)}, u32[]{:S(2)}, u32[]{:S(2)}) collective-permute-start(bf16[32,1024]{1,0:T(8,128)(2,1)S(1)} %add_convert_fusion.2), channel_id=1, source_target_pairs={{8,0},{16,8},{24,16},{9,1},{17,9},{25,17},{10,2},{18,10},{26,18},{... | collective-permute-start | bytes 196616 | tf_op jit(solution)/shard_map/ppermute | solution.py:14
  100.5 18.5 %all-to-all-start.3 = ((bf16[8,32,1024]{2,1,0:T(8,128)(2,1)}), bf16[8,32,1024]{2,1,0:T(8,128)(2,1)S(1)}, u32[]{:S(2)}, u32[]{:S(2)}) async-start(bf16[8,32,1024]{2,1,0:T(8,128)(2,1)} %broadcast_in_dim.18), calls=%async_computation.3 | async-start | bytes 1048576 | tf_op jit(solution)/shard_map/all_to_all | solution.py:27
  133.3 19.9 %all-to-all-start.4 = ((bf16[8,32,1024]{2,1,0:T(8,128)(2,1)}), bf16[8,32,1024]{2,1,0:T(8,128)(2,1)}, u32[]{:S(2)}, u32[]{:S(2)}) async-start(bf16[8,32,1024]{2,1,0:T(8,128)(2,1)} %bitcast.165), calls=%async_computation.4 | async-start | bytes 1048576 | tf_op jit(solution)/shard_map/all_to_all | solution.py:67
  145.7 11.9 %copy-start.22 = (bf16[2,32,1024]{2,1,0:T(8,128)(2,1)S(1)}, bf16[2,32,1024]{2,1,0:T(8,128)(2,1)}, u32[]{:S(2)}) copy-start(bf16[2,32,1024]{2,1,0:T(8,128)(2,1)} %param.11) | copy-start | bytes 393220
  154.4 3.1 %collective-permute-start.1 = (bf16[32,1024]{1,0:T(8,128)(2,1)S(1)}, bf16[32,1024]{1,0:T(8,128)(2,1)S(1)}, u32[]{:S(2)}, u32[]{:S(2)}) collective-permute-start(bf16[32,1024]{1,0:T(8,128)(2,1)S(1)} %add_convert_fusion.1), channel_id=1, source_target_pairs={{8,0},{16,8},{24,16},{9,1},{17,9},{25,17},{10,2},{18,10},{26,18},{... | collective-permute-start | bytes 196616 | tf_op jit(solution)/shard_map/ppermute | solution.py:14
  158.5 18.3 %all-to-all-start.5 = ((bf16[8,32,1024]{2,1,0:T(8,128)(2,1)}), bf16[8,32,1024]{2,1,0:T(8,128)(2,1)S(1)}, u32[]{:S(2)}, u32[]{:S(2)}) async-start(bf16[8,32,1024]{2,1,0:T(8,128)(2,1)} %broadcast_in_dim.19), calls=%async_computation.5 | async-start | bytes 1048576 | tf_op jit(solution)/shard_map/all_to_all | solution.py:27
  186.7 12.0 %all-to-all-start.6 = ((f32[8,3,2]{1,2,0:T(2,128)}), f32[8,3,2]{1,2,0:T(2,128)S(1)}, u32[]{:S(2)}, u32[]{:S(2)}) async-start(f32[8,3,2]{1,2,0:T(2,128)} %broadcast_in_dim.20), calls=%async_computation.6 | async-start | bytes 16384 | tf_op jit(solution)/shard_map/all_to_all | solution.py:27
  198.7 27.3 %all-to-all-start.7 = ((bf16[8,32,1024]{2,1,0:T(8,128)(2,1)}), bf16[8,32,1024]{2,1,0:T(8,128)(2,1)}, u32[]{:S(2)}, u32[]{:S(2)}) async-start(bf16[8,32,1024]{2,1,0:T(8,128)(2,1)} %bitcast.163), calls=%async_computation.7 | async-start | bytes 1048576 | tf_op jit(solution)/shard_map/all_to_all | solution.py:67
  205.1 11.4 %copy-start.2 = (bf16[256,4096]{1,0:T(8,128)(2,1)S(1)}, bf16[256,4096]{1,0:T(8,128)(2,1)}, u32[]{:S(2)}) copy-start(bf16[256,4096]{1,0:T(8,128)(2,1)} %copy-done.1) | copy-start | bytes 6291460
  205.1 11.4 %copy-start.5 = (bf16[256,4096]{1,0:T(8,128)(2,1)S(1)}, bf16[256,4096]{1,0:T(8,128)(2,1)}, u32[]{:S(2)}) copy-start(bf16[256,4096]{1,0:T(8,128)(2,1)} %copy-done.4) | copy-start | bytes 6291460
  205.1 11.4 %copy-start.7 = (bf16[8,32,1024]{2,1,0:T(8,128)(2,1)S(1)}, bf16[8,32,1024]{2,1,0:T(8,128)(2,1)}, u32[]{:S(2)}) copy-start(bf16[8,32,1024]{2,1,0:T(8,128)(2,1)} %copy-done.6) | copy-start | bytes 1572868
  205.1 11.4 %copy-start.11 = (bf16[8,32,1024]{2,1,0:T(8,128)(2,1)S(1)}, bf16[8,32,1024]{2,1,0:T(8,128)(2,1)}, u32[]{:S(2)}) copy-start(bf16[8,32,1024]{2,1,0:T(8,128)(2,1)} %copy-done.9) | copy-start | bytes 1572868
  205.1 11.4 %copy-start.13 = (bf16[8,32,1024]{2,1,0:T(8,128)(2,1)S(1)}, bf16[8,32,1024]{2,1,0:T(8,128)(2,1)}, u32[]{:S(2)}) copy-start(bf16[8,32,1024]{2,1,0:T(8,128)(2,1)} %get-tuple-element.16) | copy-start | bytes 1572868
  216.5 10.6 %copy-start.16 = (bf16[32,1024]{1,0:T(8,128)(2,1)S(1)}, bf16[32,1024]{1,0:T(8,128)(2,1)}, u32[]{:S(2)}) copy-start(bf16[32,1024]{1,0:T(8,128)(2,1)} %copy-done.15) | copy-start | bytes 196612
  216.5 10.6 %copy-start.20 = (bf16[32,1024]{1,0:T(8,128)(2,1)S(1)}, bf16[32,1024]{1,0:T(8,128)(2,1)}, u32[]{:S(2)}) copy-start(bf16[32,1024]{1,0:T(8,128)(2,1)} %copy-done.19) | copy-start | bytes 196612
  216.5 10.6 %copy-start.21 = (bf16[1,32,1024]{2,1,0:T(8,128)(2,1)S(1)}, bf16[1,32,1024]{2,1,0:T(8,128)(2,1)}, u32[]{:S(2)}) copy-start(bf16[1,32,1024]{2,1,0:T(8,128)(2,1)} %fusion.79) | copy-start | bytes 196612
  (20 other events, 85.8 us)
